TPU v7x, 128 devices: a whole 4x4x4 slice. The times are simulated.
128 devices in a mesh: dp: 32 (over z, x, core), rep: 4 (over y).
Axes of the slice: x: 4, y: 4, z: 4, core: 2. Of those that a mesh axis runs over, the one named last changes fastest.
Arguments:
- token_inputs: bfloat16 [65536, 2048], P(('dp', 'rep')), may hold values from -12 to 12
- cotangent: bfloat16 [65536, 2048], P(('dp', 'rep')), may hold values from -24 to 24
- gate_preact: bfloat16 [65536, 768], P(('dp', 'rep')), may hold values from -6 to 6
- up_preact: bfloat16 [65536, 768], P(('dp', 'rep')), may hold values from -6 to 6
- down_weight: bfloat16 [2, 768, 2048], P(None, None, 'dp'), may hold values from -0.21875 to 0.21875
- block_expert: int32 [512], P(('dp', 'rep')), may hold values from 0 to 1
- block_count: int32 [512], P(('dp', 'rep')), may hold values from 1 to 128, as said below
Outputs:
- update: bfloat16 [2, 3, 768, 2048], P(None, None, None, 'dp')
Inputs may be any that keep to these rules, and one draw needn't show every extreme that they name: `block_count`: live rows of a block, at most 128; in every draw some block is full.
All inputs are finite; a program needn't handle non-finite values.
Results may differ from a plain program's by a relative error of at most 0.02.
Values may be sent and summed in bfloat16 or wider, within the bound.
No kernel may reach another device: no remote copies, remote signals or barrier semaphores. Data moves between devices by JAX's collectives and lax.ppermute only.
A program may use at most 128 MiB of HBM per device.

v0:
```python
import math
import jax
import jax.numpy as jnp
from jax import lax
from jax.sharding import Mesh
from jax.sharding import PartitionSpec as P

D = 2048
ITERS = 2
DP = ("dp_0", "dp_1", "dp_2")
DP_REP = ("dp_0", "dp_1", "dp_2", "rep")
ns_first = 3.4445
ns_second = -4.775
ns_third = 2.0315
norm_eps = 1e-07


def cut_along(value, dim, count):
    shape = value.shape
    blocks = value.reshape(*shape[:dim], count, shape[dim] // count, *shape[dim + 1 :])
    return jnp.moveaxis(blocks, dim, 0)


def sum_by_chip(value, chips, core, dim):
    sizes = (lax.axis_size(chips), lax.axis_size(core))
    blocks = cut_along(value, dim, sizes[0] * sizes[1])
    inside = blocks.shape[1:]
    blocks = blocks.reshape(*sizes, *inside).swapaxes(0, 1).reshape(-1, *inside)
    blocks = lax.psum_scatter(blocks, core, scatter_dimension=0, tiled=True)
    return lax.psum_scatter(blocks, chips, scatter_dimension=0, tiled=True)[0]


def copy_for_each(value, axis):
    count = lax.axis_size(axis)
    return lax.all_to_all(
        jnp.broadcast_to(value[None], (count, *value.shape)), axis, 0, 0, tiled=True
    )


def of_everyone(value, axis):
    everything = copy_for_each(value, axis)
    return jnp.sum(everything.astype(jnp.float32), axis=0)


def taken_together(value, axis):
    everything = copy_for_each(value, axis)
    return jnp.sum(everything, axis=0)


def whole_sweeps(matrix, column_width, groups_all, sweeps, scale):
    hidden_width = matrix.shape[0]
    group = math.gcd(8, groups_all)
    current = matrix
    result = None
    for sweep in range(sweeps):

        def add_group(index, total):
            cols = lax.dynamic_slice_in_dim(
                current, index * group * column_width, group * column_width, 1
            )
            cols = cols.reshape(hidden_width, group, column_width)
            term = jnp.einsum(
                "fnd,gnd->nfg", cols, cols, preferred_element_type=jnp.float32
            ).astype(jnp.bfloat16)
            return total + jnp.sum(lax.optimization_barrier(term).astype(jnp.float32), axis=0)

        gram = lax.fori_loop(
            0, groups_all // group, add_group, jnp.zeros((hidden_width, hidden_width), jnp.float32)
        )
        gram_half = gram.astype(jnp.bfloat16)
        squared = jnp.dot(gram_half, gram_half, preferred_element_type=jnp.float32)
        poly = (ns_second * gram + ns_third * squared).astype(jnp.bfloat16)
        newer = ns_first * current.astype(jnp.float32) + jnp.dot(
            poly, current, preferred_element_type=jnp.float32
        )
        if sweep + 1 < sweeps:
            current = newer.astype(jnp.bfloat16)
        else:
            result = (scale * newer).astype(jnp.bfloat16)
    return result


def per_device(
    token_inputs, cotangent, gate_preact, up_preact, down_weight, block_expert, block_count
):
    blocks = block_count.shape[0]
    rows_here = token_inputs.shape[0]
    hidden_width = gate_preact.shape[1]
    width = token_inputs.shape[1]
    block_rows = rows_here // blocks
    experts_here = down_weight.shape[0]
    row_place = jnp.arange(rows_here, dtype=jnp.int32) % block_rows
    row_count = jnp.repeat(block_count, block_rows, total_repeat_length=rows_here)
    row_expert = jnp.repeat(block_expert, block_rows, total_repeat_length=rows_here)
    live_rows = row_place < row_count
    masked = jnp.where(live_rows[:, None], cotangent, jnp.zeros_like(cotangent))
    gate = gate_preact.astype(jnp.float32)
    upper = up_preact.astype(jnp.float32)
    sigmoid_gate = jax.nn.sigmoid(gate)
    hidden = (gate * sigmoid_gate * upper).astype(jnp.bfloat16)
    selector = (row_expert[None, :] == jnp.arange(experts_here, dtype=jnp.int32)[:, None]).astype(
        jnp.bfloat16
    )
    masked_each = masked[None, :, :] * selector[:, :, None]
    weights_all = lax.all_gather(down_weight, DP, axis=2, tiled=True)
    back = jnp.einsum("erd,efd->rf", masked_each, weights_all, preferred_element_type=jnp.float32)
    grad_gate = (back * upper * sigmoid_gate * (1.0 + gate * (1.0 - sigmoid_gate))).astype(
        jnp.bfloat16
    )
    grad_up = (back * gate * sigmoid_gate).astype(jnp.bfloat16)
    gate_up = jnp.concatenate([grad_gate, grad_up], axis=1)
    gate_up_each = gate_up[None, :, :] * selector[:, :, None]
    hidden_each = hidden[None, :, :] * selector[:, :, None]
    input_part = jnp.einsum(
        "erf,rd->efd", gate_up_each, token_inputs, preferred_element_type=jnp.float32
    )
    output_part = jnp.einsum("erf,rd->efd", hidden_each, masked, preferred_element_type=jnp.float32)
    partial_value = jnp.concatenate(
        [input_part.reshape(experts_here, 2, hidden_width, width), output_part[:, None]], axis=1
    )
    partial_half = partial_value.astype(jnp.bfloat16)
    terms = lax.optimization_barrier(partial_half).astype(jnp.float32)
    grad = sum_by_chip(terms.astype(jnp.bfloat16), ("dp_0", "dp_1"), "dp_2", 3).astype(jnp.float32)
    grad = of_everyone(grad.astype(jnp.bfloat16), "rep").astype(jnp.float32)
    squares = taken_together(jnp.sum(grad * grad, axis=(2, 3)), DP)
    current = (grad / (jnp.sqrt(squares) + norm_eps)[:, :, None, None]).astype(jnp.bfloat16)
    column_width = current.shape[3]
    scale = jnp.sqrt(jnp.float32(D))
    result = None
    n_dp = lax.axis_size(DP)
    matrices = experts_here * 3
    flat = current.reshape(matrices, hidden_width, column_width)
    padding = jnp.zeros((n_dp - matrices, hidden_width, column_width), jnp.bfloat16)
    outbound = jnp.concatenate([flat, padding], axis=0)
    owned = lax.all_to_all(outbound, DP, split_axis=0, concat_axis=2, tiled=True)
    finished = whole_sweeps(owned[0], column_width, n_dp, ITERS, scale)
    returned = lax.all_to_all(finished[None], DP, split_axis=2, concat_axis=0, tiled=True)
    result = returned[:matrices].reshape(experts_here, 3, hidden_width, column_width)
    return result


def solution(mesh):
    torus = Mesh(mesh.devices.reshape(4, 4, 2, mesh.shape["rep"]), ("dp_0", "dp_1", "dp_2", "rep"))
    return jax.shard_map(
        per_device,
        mesh=torus,
        in_specs=(
            P(DP_REP, None),
            P(DP_REP, None),
            P(DP_REP, None),
            P(DP_REP, None),
            P(None, None, DP),
            P(DP_REP),
            P(DP_REP),
        ),
        out_specs=P(None, None, None, DP),
        check_vma=False,
    )
```

profile of v0, /device:TPU:1, one launch (start us, length us, event | category | flops | bytes accessed | tf_op | source)
XLA Modules:
  0.0 566.8 jit_solution(1773095210929279019)
XLA Ops:
  7.3 1.4 fusion.42
  8.7 2.5 fusion.30
  11.2 1.4 fusion.41
  12.6 2.5 select_select_fusion
  15.2 3.2 broadcast_select_fusion
  18.3 44.0 %all-gather.2.cloned.1.call-done = bf16[2,768,2048]{1,2,0:T(8,128)(2,1)} async-done(((bf16[2,768,64]{1,2,0:T(8,128)(2,1)}), bf16[2,768,2048]{1,2,0:T(8,128)(2,1)}) %all-gather.2.cloned.1.call-update) | async-done | bytes 6291472 | tf_op jit(solution)/shard_map/all_gather | solution.py:105
  62.4 7.8 %fusion.10 = (bf16[512,768]{1,0:T(8,128)(2,1)S(1)}, bf16[512,768]{1,0:T(8,128)(2,1)S(1)}, bf16[512,768]{1,0:T(8,128)(2,1)S(1)}) fusion(bf16[512,768]{1,0:T(8,128)(2,1)} %param.20, bf16[512,768]{1,0:T(8,128)(2,1)} %param.19, bf16[2,768,2048]{1,2,0:T(8,128)(2,1)} %all-gather.2.cloned.1.call-done, bf16[2,512]{1,0:T(2,128)(2,1)S(1)} %compare_convert_fusion, ...), kind=kOutput, calls=%fused_computation.33 | convolution fusion | flops 3230400512 | bytes 12322816 | tf_op jit(solution)/shard_map/erd,efd->rf/dot_general | solution.py:106
  70.2 1.3 pad_maximum_fusion.1
  71.4 2.6 copy.51
  74.0 10.6 %convolution_convert_fusion.2 = bf16[2,1536,2048]{2,1,0:T(8,128)(2,1)} fusion(bf16[512,2048]{1,0:T(8,128)(2,1)S(1)} %copy-done, bf16[2,512]{1,0:T(2,128)(2,1)S(1)} %compare_convert_fusion, bf16[512,1536]{0,1:T(8,128)(2,1)} %copy.51), kind=kOutput, calls=%fused_computation.9 | convolution fusion | flops 6450315264 | bytes 16254976 | tf_op jit(solution)/shard_map/erf,rd->efd/dot_general | solution.py:114
  84.7 16.8 %copy.53 = bf16[2,2,768,2048]{2,3,1,0:T(8,128)(2,1)} copy(bf16[2,2,768,2048]{3,2,1,0:T(8,128)(2,1)} %bitcast.100) | data formatting | bytes 25165824 | tf_op jit(solution)/shard_map/reshape | solution.py:119
  101.4 1.2 copy.52
  102.6 6.3 %convert_bitcast_fusion = bf16[2,1,768,2048]{3,2,0,1:T(8,128)(2,1)} fusion(bf16[512,2048]{1,0:T(8,128)(2,1)S(1)} %copy-done.2, bf16[2,512]{1,0:T(2,128)(2,1)S(1)} %compare_convert_fusion, bf16[512,768]{0,1:T(8,128)(2,1)} %copy.52), kind=kOutput, calls=%fused_computation.12 | convolution fusion | flops 3225157632 | bytes 9177088 | tf_op jit(solution)/shard_map/erf,rd->efd/dot_general | solution.py:117
  108.9 8.7 %copy.54 = bf16[2,1,768,2048]{2,3,1,0:T(8,128)(2,1)} copy(bf16[2,1,768,2048]{3,2,0,1:T(8,128)(2,1)} %convert_bitcast_fusion) | data formatting | bytes 12582912 | tf_op jit(solution)/shard_map/broadcast_in_dim | solution.py:119
  117.6 9.5 %pad_maximum_fusion = bf16[2,3,768,2048]{2,3,1,0:T(8,128)(2,1)S(1)} fusion(bf16[2,1,768,2048]{2,3,1,0:T(8,128)(2,1)} %copy.54, bf16[2,2,768,2048]{2,3,1,0:T(8,128)(2,1)} %copy.53), kind=kLoop, calls=%fused_computation.8 | loop fusion | flops 9437184 | bytes 37748736 | tf_op jit(solution)/shard_map/concatenate | solution.py:118
  127.1 6.7 %copy.55 = bf16[16,2,2,3,768,64]{4,5,3,2,0,1:T(8,128)(2,1)} copy(bf16[16,2,2,3,768,64]{4,5,1,0,3,2:T(8,128)(2,1)S(1)} %bitcast.97) | data formatting | bytes 37748736 | tf_op jit(solution)/shard_map/reshape | solution.py:28
  133.9 28.0 %reduce-scatter.5.cloned.1.call-done = bf16[16,2,3,768,64]{3,4,2,1,0:T(8,128)(2,1)} async-done(((bf16[32,2,3,768,64]{3,4,2,1,0:T(8,128)(2,1)}), bf16[16,2,3,768,64]{3,4,2,1,0:T(8,128)(2,1)}) %reduce-scatter.5.cloned.1.call-update) | async-done | bytes 9437200 | tf_op jit(solution)/shard_map/reduce_scatter | solution.py:29
  161.9 91.3 %reduce-scatter.7.cloned.1.call-done = bf16[1,2,3,768,64]{3,4,2,1,0:T(8,128)(2,1)} async-done(((bf16[16,2,3,768,64]{3,4,2,1,0:T(8,128)(2,1)}), bf16[1,2,3,768,64]{3,4,2,1,0:T(8,128)(2,1)}) %reduce-scatter.7.cloned.1.call-update) | async-done | bytes 589840
  253.2 1.3 broadcast_in_dim.31
  254.5 30.7 %all_to_all.40 = bf16[4,2,3,768,64]{3,4,2,1,0:T(8,128)(2,1)S(1)} all-to-all(bf16[4,2,3,768,64]{3,4,2,1,0:T(8,128)(2,1)S(1)} %broadcast_in_dim.31), channel_id=1, replica_groups=mesh['dp_0'=4,'dp_1'=4,'dp_2'=2,'rep'=4] {'rep'}, dimensions={0} | all-to-all | bytes 4718592 | tf_op jit(solution)/shard_map/all_to_all | solution.py:35
  285.8 15.0 %all_to_all.41 = f32[32,2,3]{2,1,0:T(2,128)S(1)} all-to-all(f32[32,2,3]{2,1,0:T(2,128)S(1)} %broadcast_in_dim.32), channel_id=1, replica_groups=mesh['dp_0'=4,'dp_1'=4,'dp_2'=2,'rep'=4] {'dp_0','dp_1','dp_2'}, dimensions={0} | all-to-all | bytes 1536 | tf_op jit(solution)/shard_map/all_to_all | solution.py:35
  301.3 2.0 concatenate.18
  303.3 5.0 all-to-all-start.2
  308.3 39.9 %all-to-all-done.2 = bf16[32,768,64]{1,2,0:T(8,128)(2,1)} async-done(((bf16[32,768,64]{1,2,0:T(8,128)(2,1)}), bf16[32,768,64]{1,2,0:T(8,128)(2,1)}, u32[]{:S(2)}, u32[]{:S(2)}) %all-to-all-start.2) | async-done | bytes 3145760 | tf_op jit(solution)/shard_map/all_to_all | solution.py:135
  348.2 4.7 copy.58
  352.9 33.6 %while.34 = (s32[]{:T(128)}, f32[768,768]{1,0:T(8,128)}, bf16[768,2048]{0,1:T(8,128)(2,1)}, s32[]{:T(128)}, s32[]{:T(128)}, /*index=5*/s32[]{:T(128)}, s32[]{:T(128)}) while((s32[]{:T(128)}, f32[768,768]{1,0:T(8,128)}, bf16[768,2048]{0,1:T(8,128)(2,1)}, s32[]{:T(128)}, s32[]{:T(128)}, /*index=5*/s32[]{:T(128)}, s32[]{:T(128)}) %tuple.98), condition=%wide.region_7.9_spmd.clone, body=%wide.region_5.8_spmd.clone.sunk | while | flops 618725376 | bytes 30670984 | solution.py:67
  352.9 1.2 constant_dynamic-slice_fusion.4
  354.1 2.9 convolution_convert_fusion.5
  357.0 1.2 convert_reduce_fusion.5
  358.3 1.8 select_add_fusion.4
  360.1 1.2 constant_dynamic-slice_fusion.4
  361.3 2.9 convolution_convert_fusion.5
  364.2 1.2 convert_reduce_fusion.5
  365.4 3.4 select_add_fusion.4
  368.9 1.2 constant_dynamic-slice_fusion.4
  370.1 2.9 convolution_convert_fusion.5
  373.0 1.2 convert_reduce_fusion.5
  374.2 3.4 select_add_fusion.4
  377.7 1.2 constant_dynamic-slice_fusion.4
  378.9 2.9 convolution_convert_fusion.5
  381.8 1.2 convert_reduce_fusion.5
  383.0 3.4 select_add_fusion.4
  386.5 10.5 %add_convert_fusion = bf16[768,2048]{1,0:T(8,128)(2,1)} fusion(bf16[768,2048]{1,0:T(8,128)(2,1)} %copy.58, bf16[768,2048]{0,1:T(8,128)(2,1)} %bitcast.23, f32[768,768]{1,0:T(8,128)} %get-tuple-element.202), kind=kOutput, calls=%fused_computation.11 | convolution fusion | flops 3331129344 | bytes 11796480 | tf_op jit(solution)/shard_map/dot_general | solution.py:73
  397.0 34.4 %while.35 = (s32[]{:T(128)}, f32[768,768]{1,0:T(8,128)}, bf16[768,2048]{1,0:T(8,128)(2,1)}, s32[]{:T(128)}, s32[]{:T(128)}, /*index=5*/s32[]{:T(128)}, s32[]{:T(128)}) while((s32[]{:T(128)}, f32[768,768]{1,0:T(8,128)}, bf16[768,2048]{1,0:T(8,128)(2,1)}, s32[]{:T(128)}, s32[]{:T(128)}, /*index=5*/s32[]{:T(128)}, s32[]{:T(128)}) %tuple.101), condition=%wide.region_10.12_spmd.clone, body=%wide.region_8.11_spmd.clone.sunk | while | flops 618725376 | bytes 32243848 | solution.py:67
  397.0 1.2 constant_dynamic-slice_fusion.5
  398.4 2.9 convolution_convert_fusion.6
  401.3 1.2 convert_reduce_fusion.6
  402.6 1.7 select_add_fusion.5
  405.8 2.9 convolution_convert_fusion.6
  408.7 1.2 convert_reduce_fusion.6
  410.0 3.4 select_add_fusion.5
  414.8 2.9 convolution_convert_fusion.6
  417.7 1.2 convert_reduce_fusion.6
  419.0 3.4 select_add_fusion.5
  423.8 2.9 convolution_convert_fusion.6
  426.7 1.2 convert_reduce_fusion.6
  428.0 3.4 select_add_fusion.5
  431.4 8.5 %fusion.3 = bf16[1,768,2048]{2,1,0:T(8,128)(2,1)S(1)} fusion(bf16[768,2048]{1,0:T(8,128)(2,1)} %get-tuple-element.360, f32[768,768]{1,0:T(8,128)} %get-tuple-element.203), kind=kOutput, calls=%fused_computation.17 | convolution fusion | flops 3332702208 | bytes 8650752 | tf_op jit(solution)/shard_map/dot_general | solution.py:73
  439.9 11.2 %copy.60 = bf16[1,768,2048]{1,0,2:T(2,128)(2,1)} copy(bf16[1,768,2048]{2,1,0:T(8,128)(2,1)S(1)} %fusion.3) | data formatting | bytes 6291456 | tf_op jit(solution)/shard_map/broadcast_in_dim | solution.py:137
  451.7 33.3 %reduce.3 = bf16[2048,768]{1,0:T(8,128)(2,1)} reduce(bf16[2048,1,768]{2,1,0:T(2,128)(2,1)} %bitcast.98, bf16[]{:T(256)} %broadcast.220), dimensions={1}, to_apply=%bitcast.73.reduce_sub_computation | reduce | bytes 6291458
  485.0 6.6 %reshape.174 = bf16[32,2,24576]{2,1,0:T(2,128)(2,1)S(1)} reshape(bf16[2048,768]{1,0:T(8,128)(2,1)} %reduce.3) | data formatting | bytes 6291456
  491.6 45.5 %all_to_all.42 = bf16[32,2,24576]{2,1,0:T(2,128)(2,1)} all-to-all(bf16[32,2,24576]{2,1,0:T(2,128)(2,1)S(1)} %reshape.174), channel_id=1, replica_groups=mesh['dp_0'=4,'dp_1'=4,'dp_2'=2,'rep'=4] {'dp_0','dp_1','dp_2'}, dimensions={0} | all-to-all | bytes 6291456 | tf_op jit(solution)/shard_map/all_to_all | solution.py:137
  537.1 18.9 %reshape.175 = bf16[2048,1,768]{2,1,0:T(2,128)(2,1)} reshape(bf16[32,2,24576]{2,1,0:T(2,128)(2,1)} %all_to_all.42) | data formatting | bytes 6291456
  556.0 3.5 copy.62
  (33 shorter events, 7.9 us)
Async XLA Ops:
  6.5 67.5 %copy-start = (bf16[512,2048]{1,0:T(8,128)(2,1)S(1)}, bf16[512,2048]{1,0:T(8,128)(2,1)}, u32[]{:S(2)}) copy-start(bf16[512,2048]{1,0:T(8,128)(2,1)} %param.17) | copy-start | bytes 6291460
  6.5 55.8 %all-gather.2.cloned.1.call-start = ((), (), s32[]{:S(2)}) async-start(), calls=%async_computation.6 | async-start | bytes 6488064 | tf_op jit(solution)/shard_map/all_gather | solution.py:105
  7.3 154.6 %reduce-scatter.5.cloned.1.call-start = ((), (), s32[]{:S(2)}) async-start(), calls=%async_computation.7 | async-start | bytes 28311552 | tf_op jit(solution)/shard_map/reduce_scatter | solution.py:29
  84.7 18.0 %copy-start.2 = (bf16[512,2048]{1,0:T(8,128)(2,1)S(1)}, bf16[512,2048]{1,0:T(8,128)(2,1)}, u32[]{:S(2)}) copy-start(bf16[512,2048]{1,0:T(8,128)(2,1)} %broadcast_select_fusion) | copy-start | bytes 6291460
  133.8 119.4 %reduce-scatter.7.cloned.1.call-start = ((), (), s32[]{:S(2)}) async-start(), calls=%async_computation.8 | async-start | bytes 10027008
  303.3 44.9 %all-to-all-start.2 = ((bf16[32,768,64]{1,2,0:T(8,128)(2,1)}), bf16[32,768,64]{1,2,0:T(8,128)(2,1)}, u32[]{:S(2)}, u32[]{:S(2)}) async-start(bf16[32,768,64]{1,2,0:T(8,128)(2,1)} %concatenate.18), calls=%async_computation.3 | async-start | bytes 6291456 | tf_op jit(solution)/shard_map/all_to_all | solution.py:135
  556.0 4.3 copy-start.1
Sparse Core Ops, SparseCore 0:
  9.6 52.6 all-gather.1
  133.9 27.9 reduce-scatter.4
  165.4 87.7 reduce-scatter.6
where the time goes:
time: 570 us; the launch traced here: 567 us
  waiting for transfers between devices  204 us (36%)
  local copies, waits for them, and re-layouts  99.3 us (17%)
  blocking collectives  91.1 us (16%)
  other arithmetic  87 us (15%)
  matrix products  66.9 us (12%)
  between operations  13.2 us (2%)
    unnamed x4, waiting for transfers between devices  92 us
    all_to_all x2, blocking collectives, copy_for_each(): lax.all_to_all(jnp.broadcast_to(value[None], (count, *value.shape)), axis...  45.6 us
    all_to_all x1, blocking collectives, per_device(): lax.all_to_all(finished[None], DP, split_axis=2, concat_axis=0, tiled=True)  45.5 us
    all_gather x1, waiting for transfers between devices, per_device(): weights_all = lax.all_gather(down_weight, DP, axis=2, tiled=True)  44 us
    all_to_all x1, waiting for transfers between devices, per_device(): lax.all_to_all(outbound, DP, split_axis=0, concat_axis=2, tiled=True)  39.9 us
    unnamed x3, other arithmetic  33.3 us
    unnamed x11, local copies, waits for them, and re-layouts  29.6 us
    reduce_scatter x1, waiting for transfers between devices, sum_by_chip(): blocks = lax.psum_scatter(blocks, core, scatter_dimension=0, tiled=True)  28 us
  transfers between devices with their start and end apart: 4, of which 4 were waited for; matrix products, arithmetic and copies ran while one was open for 2% of the time, Pallas kernels for 0%

commit v1 on v0

--- a/solution.py
+++ b/solution.py
@@ -13,6 +13,12 @@
 ns_second = -4.775
 ns_third = 2.0315
 norm_eps = 1e-07
+
+
+def trade_parts(value, name, split, join):
+    pieces = jnp.split(value, lax.axis_size(name), axis=split)
+    arrived = lax.all_to_all(jnp.stack(pieces), name, 0, 0)
+    return jnp.concatenate(arrived, axis=join)
 
 
 def cut_along(value, dim, count):
@@ -134,7 +140,7 @@
     outbound = jnp.concatenate([flat, padding], axis=0)
     owned = lax.all_to_all(outbound, DP, split_axis=0, concat_axis=2, tiled=True)
     finished = whole_sweeps(owned[0], column_width, n_dp, ITERS, scale)
-    returned = lax.all_to_all(finished[None], DP, split_axis=2, concat_axis=0, tiled=True)
+    returned = trade_parts(finished[None], DP, 2, 0)
     result = returned[:matrices].reshape(experts_here, 3, hidden_width, column_width)
     return result
 

time: 570 us -> 527 us (0.925)
  other arithmetic: 87 us -> 53.7 us
  local copies, waits for them, and re-layouts: 99.3 us -> 90.1 us
    unnamed x3 -> x2, other arithmetic: 33.3 us -> 0.01 us
    broadcast_in_dim x1 -> x0, local copies, waits for them, and re-layouts: 11.2 us -> none  [per_device(): finished[None]]
    another operation x0 -> x2, local copies, waits for them, and re-layouts: none -> 7.79 us  [trade_parts(): arrived = lax.all_to_all(jnp.stack(pieces), name, 0, 0)]
    unnamed x11 -> x38, local copies, waits for them, and re-layouts: 29.6 us -> 23.8 us
where the time goes in v1:
time: 527 us; the launch traced here: 525 us
  waiting for transfers between devices  204 us (39%)
  blocking collectives  91.5 us (17%)
  local copies, waits for them, and re-layouts  90.1 us (17%)
  matrix products  66.9 us (13%)
  other arithmetic  53.7 us (10%)
  between operations  13.2 us (3%)
    unnamed x4, waiting for transfers between devices  92 us
    all_to_all x1, blocking collectives, trade_parts(): arrived = lax.all_to_all(jnp.stack(pieces), name, 0, 0)  45.8 us
    all_to_all x2, blocking collectives, copy_for_each(): lax.all_to_all(jnp.broadcast_to(value[None], (count, *value.shape)), axis...  45.6 us
    all_gather x1, waiting for transfers between devices, per_device(): weights_all = lax.all_gather(down_weight, DP, axis=2, tiled=True)  44 us
    all_to_all x1, waiting for transfers between devices, per_device(): lax.all_to_all(outbound, DP, split_axis=0, concat_axis=2, tiled=True)  39.9 us
    reduce_scatter x1, waiting for transfers between devices, sum_by_chip(): blocks = lax.psum_scatter(blocks, core, scatter_dimension=0, tiled=True)  28 us
    add x8, other arithmetic, add_group(): total + jnp.sum(lax.optimization_barrier(term).astype(jnp.float32), axis=0)  24 us
    unnamed x38, local copies, waits for them, and re-layouts  23.8 us
  transfers between devices with their start and end apart: 4, of which 4 were waited for; matrix products, arithmetic and copies ran while one was open for 2% of the time, Pallas kernels for 0%

profile of v1, /device:TPU:1, one launch (start us, length us, event | category | flops | bytes accessed | tf_op | source)
XLA Modules:
  0.0 524.7 jit_solution(4073043127617027436)
XLA Ops:
  7.3 1.4 fusion.74
  8.7 2.5 fusion.62
  11.2 1.4 fusion.73
  12.6 2.5 select_select_fusion
  15.2 3.2 broadcast_select_fusion
  18.3 44.0 %all-gather.2.cloned.1.call-done = bf16[2,768,2048]{1,2,0:T(8,128)(2,1)} async-done(((bf16[2,768,64]{1,2,0:T(8,128)(2,1)}), bf16[2,768,2048]{1,2,0:T(8,128)(2,1)}) %all-gather.2.cloned.1.call-update) | async-done | bytes 6291472 | tf_op jit(solution)/shard_map/all_gather | solution.py:111
  62.4 7.8 %fusion.10 = (bf16[512,768]{1,0:T(8,128)(2,1)S(1)}, bf16[512,768]{1,0:T(8,128)(2,1)S(1)}, bf16[512,768]{1,0:T(8,128)(2,1)S(1)}) fusion(bf16[512,768]{1,0:T(8,128)(2,1)} %param.20, bf16[512,768]{1,0:T(8,128)(2,1)} %param.19, bf16[2,768,2048]{1,2,0:T(8,128)(2,1)} %all-gather.2.cloned.1.call-done, bf16[2,512]{1,0:T(2,128)(2,1)S(1)} %compare_convert_fusion, ...), kind=kOutput, calls=%fused_computation.33 | convolution fusion | flops 3230400512 | bytes 12322816 | tf_op jit(solution)/shard_map/erd,efd->rf/dot_general | solution.py:112
  70.2 1.3 pad_maximum_fusion.1
  71.4 2.6 copy.51
  74.0 10.6 %convolution_convert_fusion.2 = bf16[2,1536,2048]{2,1,0:T(8,128)(2,1)} fusion(bf16[512,2048]{1,0:T(8,128)(2,1)S(1)} %copy-done, bf16[2,512]{1,0:T(2,128)(2,1)S(1)} %compare_convert_fusion, bf16[512,1536]{0,1:T(8,128)(2,1)} %copy.51), kind=kOutput, calls=%fused_computation.9 | convolution fusion | flops 6450315264 | bytes 16254976 | tf_op jit(solution)/shard_map/erf,rd->efd/dot_general | solution.py:120
  84.7 16.8 %copy.53 = bf16[2,2,768,2048]{2,3,1,0:T(8,128)(2,1)} copy(bf16[2,2,768,2048]{3,2,1,0:T(8,128)(2,1)} %bitcast.221) | data formatting | bytes 25165824 | tf_op jit(solution)/shard_map/reshape | solution.py:125
  101.4 1.2 copy.52
  102.6 6.3 %convert_bitcast_fusion = bf16[2,1,768,2048]{3,2,0,1:T(8,128)(2,1)} fusion(bf16[512,2048]{1,0:T(8,128)(2,1)S(1)} %copy-done.2, bf16[2,512]{1,0:T(2,128)(2,1)S(1)} %compare_convert_fusion, bf16[512,768]{0,1:T(8,128)(2,1)} %copy.52), kind=kOutput, calls=%fused_computation.12 | convolution fusion | flops 3225157632 | bytes 9177088 | tf_op jit(solution)/shard_map/erf,rd->efd/dot_general | solution.py:123
  108.9 8.7 %copy.54 = bf16[2,1,768,2048]{2,3,1,0:T(8,128)(2,1)} copy(bf16[2,1,768,2048]{3,2,0,1:T(8,128)(2,1)} %convert_bitcast_fusion) | data formatting | bytes 12582912 | tf_op jit(solution)/shard_map/broadcast_in_dim | solution.py:125
  117.6 9.5 %pad_maximum_fusion = bf16[2,3,768,2048]{2,3,1,0:T(8,128)(2,1)S(1)} fusion(bf16[2,1,768,2048]{2,3,1,0:T(8,128)(2,1)} %copy.54, bf16[2,2,768,2048]{2,3,1,0:T(8,128)(2,1)} %copy.53), kind=kLoop, calls=%fused_computation.8 | loop fusion | flops 9437184 | bytes 37748736 | tf_op jit(solution)/shard_map/concatenate | solution.py:124
  127.1 6.7 %copy.55 = bf16[16,2,2,3,768,64]{4,5,3,2,0,1:T(8,128)(2,1)} copy(bf16[16,2,2,3,768,64]{4,5,1,0,3,2:T(8,128)(2,1)S(1)} %bitcast.220) | data formatting | bytes 37748736 | tf_op jit(solution)/shard_map/reshape | solution.py:34
  133.9 28.0 %reduce-scatter.5.cloned.1.call-done = bf16[16,2,3,768,64]{3,4,2,1,0:T(8,128)(2,1)} async-done(((bf16[32,2,3,768,64]{3,4,2,1,0:T(8,128)(2,1)}), bf16[16,2,3,768,64]{3,4,2,1,0:T(8,128)(2,1)}) %reduce-scatter.5.cloned.1.call-update) | async-done | bytes 9437200 | tf_op jit(solution)/shard_map/reduce_scatter | solution.py:35
  161.9 91.3 %reduce-scatter.7.cloned.1.call-done = bf16[1,2,3,768,64]{3,4,2,1,0:T(8,128)(2,1)} async-done(((bf16[16,2,3,768,64]{3,4,2,1,0:T(8,128)(2,1)}), bf16[1,2,3,768,64]{3,4,2,1,0:T(8,128)(2,1)}) %reduce-scatter.7.cloned.1.call-update) | async-done | bytes 589840
  253.2 1.3 broadcast_in_dim.31
  254.5 30.7 %all_to_all.30 = bf16[4,2,3,768,64]{3,4,2,1,0:T(8,128)(2,1)S(1)} all-to-all(bf16[4,2,3,768,64]{3,4,2,1,0:T(8,128)(2,1)S(1)} %broadcast_in_dim.31), channel_id=1, replica_groups=mesh['dp_0'=4,'dp_1'=4,'dp_2'=2,'rep'=4] {'rep'}, dimensions={0} | all-to-all | bytes 4718592 | tf_op jit(solution)/shard_map/all_to_all | solution.py:41
  285.8 15.0 %all_to_all.31 = f32[32,2,3]{2,1,0:T(2,128)S(1)} all-to-all(f32[32,2,3]{2,1,0:T(2,128)S(1)} %broadcast_in_dim.32), channel_id=1, replica_groups=mesh['dp_0'=4,'dp_1'=4,'dp_2'=2,'rep'=4] {'dp_0','dp_1','dp_2'}, dimensions={0} | all-to-all | bytes 1536 | tf_op jit(solution)/shard_map/all_to_all | solution.py:41
  301.3 2.0 concatenate.18
  303.3 5.0 all-to-all-start.2
  308.3 39.9 %all-to-all-done.2 = bf16[32,768,64]{1,2,0:T(8,128)(2,1)} async-done(((bf16[32,768,64]{1,2,0:T(8,128)(2,1)}), bf16[32,768,64]{1,2,0:T(8,128)(2,1)}, u32[]{:S(2)}, u32[]{:S(2)}) %all-to-all-start.2) | async-done | bytes 3145760 | tf_op jit(solution)/shard_map/all_to_all | solution.py:141
  348.2 4.7 copy.58
  352.9 33.6 %while.34 = (s32[]{:T(128)}, f32[768,768]{1,0:T(8,128)}, bf16[768,2048]{0,1:T(8,128)(2,1)}, s32[]{:T(128)}, s32[]{:T(128)}, /*index=5*/s32[]{:T(128)}, s32[]{:T(128)}) while((s32[]{:T(128)}, f32[768,768]{1,0:T(8,128)}, bf16[768,2048]{0,1:T(8,128)(2,1)}, s32[]{:T(128)}, s32[]{:T(128)}, /*index=5*/s32[]{:T(128)}, s32[]{:T(128)}) %tuple.98), condition=%wide.region_7.9_spmd.clone, body=%wide.region_5.8_spmd.clone.sunk | while | flops 618725376 | bytes 30670984 | solution.py:73
  352.9 1.2 constant_dynamic-slice_fusion.4
  354.1 2.9 convolution_convert_fusion.5
  357.0 1.2 convert_reduce_fusion.5
  358.3 1.8 select_add_fusion.4
  360.1 1.2 constant_dynamic-slice_fusion.4
  361.3 2.9 convolution_convert_fusion.5
  364.2 1.2 convert_reduce_fusion.5
  365.4 3.4 select_add_fusion.4
  368.9 1.2 constant_dynamic-slice_fusion.4
  370.1 2.9 convolution_convert_fusion.5
  373.0 1.2 convert_reduce_fusion.5
  374.2 3.4 select_add_fusion.4
  377.7 1.2 constant_dynamic-slice_fusion.4
  378.9 2.9 convolution_convert_fusion.5
  381.8 1.2 convert_reduce_fusion.5
  383.0 3.4 select_add_fusion.4
  386.5 10.5 %add_convert_fusion = bf16[768,2048]{1,0:T(8,128)(2,1)} fusion(bf16[768,2048]{1,0:T(8,128)(2,1)} %copy.58, bf16[768,2048]{0,1:T(8,128)(2,1)} %bitcast.23, f32[768,768]{1,0:T(8,128)} %get-tuple-element.202), kind=kOutput, calls=%fused_computation.11 | convolution fusion | flops 3331129344 | bytes 11796480 | tf_op jit(solution)/shard_map/dot_general | solution.py:79
  397.0 34.4 %while.35 = (s32[]{:T(128)}, f32[768,768]{1,0:T(8,128)}, bf16[768,2048]{1,0:T(8,128)(2,1)}, s32[]{:T(128)}, s32[]{:T(128)}, /*index=5*/s32[]{:T(128)}, s32[]{:T(128)}) while((s32[]{:T(128)}, f32[768,768]{1,0:T(8,128)}, bf16[768,2048]{1,0:T(8,128)(2,1)}, s32[]{:T(128)}, s32[]{:T(128)}, /*index=5*/s32[]{:T(128)}, s32[]{:T(128)}) %tuple.101), condition=%wide.region_10.12_spmd.clone, body=%wide.region_8.11_spmd.clone.sunk | while | flops 618725376 | bytes 32243848 | solution.py:73
  397.0 1.2 constant_dynamic-slice_fusion.5
  398.4 2.9 convolution_convert_fusion.6
  401.3 1.2 convert_reduce_fusion.6
  402.6 1.7 select_add_fusion.5
  404.3 1.2 constant_dynamic-slice_fusion.5
  405.8 2.9 convolution_convert_fusion.6
  408.7 1.2 convert_reduce_fusion.6
  410.0 3.4 select_add_fusion.5
  413.3 1.2 constant_dynamic-slice_fusion.5
  414.8 2.9 convolution_convert_fusion.6
  417.7 1.2 convert_reduce_fusion.6
  419.0 3.4 select_add_fusion.5
  422.4 1.2 constant_dynamic-slice_fusion.5
  423.8 2.9 convolution_convert_fusion.6
  426.7 1.2 convert_reduce_fusion.6
  428.0 3.4 select_add_fusion.5
  431.4 8.5 %fusion.3 = bf16[1,768,2048]{2,1,0:T(8,128)(2,1)S(1)} fusion(bf16[768,2048]{1,0:T(8,128)(2,1)} %get-tuple-element.360, f32[768,768]{1,0:T(8,128)} %get-tuple-element.203), kind=kOutput, calls=%fused_computation.17 | convolution fusion | flops 3332702208 | bytes 8650752 | tf_op jit(solution)/shard_map/dot_general | solution.py:79
  464.5 7.0 %copy.60 = bf16[32,1,768,64]{2,3,1,0:T(8,128)(2,1)} copy(bf16[32,1,768,64]{3,2,1,0:T(8,128)(2,1)} %fusion.30) | data formatting | bytes 6291456 | tf_op jit(solution)/shard_map/stack | solution.py:20
  471.5 45.8 %all_to_all.32 = bf16[32,1,768,64]{2,3,1,0:T(8,128)(2,1)S(1)} all-to-all(bf16[32,1,768,64]{2,3,1,0:T(8,128)(2,1)} %copy.60), channel_id=1, replica_groups=mesh['dp_0'=4,'dp_1'=4,'dp_2'=2,'rep'=4] {'dp_0','dp_1','dp_2'}, dimensions={0} | all-to-all | bytes 6291456 | tf_op jit(solution)/shard_map/all_to_all | solution.py:20
  517.3 0.9 slice.46
  (60 shorter events, 27.5 us)
Async XLA Ops:
  6.5 67.5 %copy-start = (bf16[512,2048]{1,0:T(8,128)(2,1)S(1)}, bf16[512,2048]{1,0:T(8,128)(2,1)}, u32[]{:S(2)}) copy-start(bf16[512,2048]{1,0:T(8,128)(2,1)} %param.17) | copy-start | bytes 6291460
  6.5 55.8 %all-gather.2.cloned.1.call-start = ((), (), s32[]{:S(2)}) async-start(), calls=%async_computation.6 | async-start | bytes 6488064 | tf_op jit(solution)/shard_map/all_gather | solution.py:111
  7.3 154.6 %reduce-scatter.5.cloned.1.call-start = ((), (), s32[]{:S(2)}) async-start(), calls=%async_computation.7 | async-start | bytes 28311552 | tf_op jit(solution)/shard_map/reduce_scatter | solution.py:35
  84.7 18.0 %copy-start.2 = (bf16[512,2048]{1,0:T(8,128)(2,1)S(1)}, bf16[512,2048]{1,0:T(8,128)(2,1)}, u32[]{:S(2)}) copy-start(bf16[512,2048]{1,0:T(8,128)(2,1)} %broadcast_select_fusion) | copy-start | bytes 6291460
  133.8 119.4 %reduce-scatter.7.cloned.1.call-start = ((), (), s32[]{:S(2)}) async-start(), calls=%async_computation.8 | async-start | bytes 10027008
  303.3 44.9 %all-to-all-start.2 = ((bf16[32,768,64]{1,2,0:T(8,128)(2,1)}), bf16[32,768,64]{1,2,0:T(8,128)(2,1)}, u32[]{:S(2)}, u32[]{:S(2)}) async-start(bf16[32,768,64]{1,2,0:T(8,128)(2,1)} %concatenate.18), calls=%async_computation.3 | async-start | bytes 6291456 | tf_op jit(solution)/shard_map/all_to_all | solution.py:141
  464.5 53.7 %copy-start.1 = (bf16[512,2048]{1,0:T(8,128)(2,1)S(1)}, bf16[512,2048]{1,0:T(8,128)(2,1)}, u32[]{:S(2)}) copy-start(bf16[512,2048]{1,0:T(8,128)(2,1)} %param.17) | copy-start | bytes 6291460
Sparse Core Ops, SparseCore 0:
  9.6 52.6 all-gather.1
  133.9 27.9 reduce-scatter.4
  165.4 87.7 reduce-scatter.6
